TPU v7x, 32 devices: a whole 2x2x4 slice. The times are simulated.
32 devices in a mesh: seq: 16 (over z, y, core), dp: 2 (over x).
Axes of the slice: x: 2, y: 2, z: 4, core: 2. Of those that a mesh axis runs over, the one named last changes fastest.
Arguments:
- acceptors: bfloat16 [2, 2048, 2560], P('dp', 'seq'), may hold values from -2 to 2
- lookups: bfloat16 [2, 2048, 2560], P('dp', 'seq'), may hold values from -0.625 to 0.625
- payloads: bfloat16 [2, 2048, 2560], P('dp', 'seq'), may hold values from -6 to 6
- lagged_fading_source: bfloat16 [2, 2048, 2560], P('dp', 'seq'), may hold values from -6 to 6
- response_cotangent: bfloat16 [2, 2048, 2560], P('dp', 'seq'), may hold values from -5 to 5
- fading_lowering_array: bfloat16 [2560, 128], replicated, may hold values from -0.125 to 0.125
- fading_raising_array: bfloat16 [2560, 128], replicated, may hold values from -1.25 to 1.25
- feature_fading_speed: float32 [2560], replicated, may hold values from 2.3251488e-05 to 0.125
- present_reward: float32 [2560], replicated, may hold values from 1.4142135 to 11.313708
Outputs:
- mixed: bfloat16 [2, 2048, 2560], P('dp', 'seq')
- grad_receptance: bfloat16 [2, 2048, 2560], P('dp', 'seq')
- lookup_deriv: bfloat16 [2, 2048, 2560], P('dp', 'seq')
- payload_deriv: bfloat16 [2, 2048, 2560], P('dp', 'seq')
- grad_decay_input: bfloat16 [2, 2048, 2560], P('dp', 'seq')
- grad_lora_a: float32 [2560, 128], P('dp')
- grad_lora_b: float32 [2560, 128], P('dp')
- grad_time_decay: float32 [2560], P('dp')
- present_reward_deriv: float32 [2560], P('dp')
All inputs are finite; a program needn't handle non-finite values.
Results may differ from a plain program's by a relative error of at most 0.006.
Values sent between devices are 32-bit elements.
A program may use at most 320 MiB of HBM per device.

v0:
```python
import jax
import jax.numpy as jnp
from jax import lax
from jax.sharding import PartitionSpec as P

ATTENDER_TOTAL = 40
LANE_TOTAL = 64
BLOCK = 64


HIGH = lax.Precision.HIGHEST


def carried_in(part, axis, combine, identity, reverse):
    count = lax.axis_size(axis)
    place = lax.axis_index(axis)
    ahead = count - 1 - place if reverse else place
    gathered = jax.tree.map(lambda a: lax.all_gather(a, axis), part)
    state = jax.tree.map(lambda a, e: jnp.zeros_like(a) + jnp.asarray(e, a.dtype), part, identity)

    def one(hop, state):
        source = count - 1 - hop if reverse else hop
        return combine(
            state, jax.tree.map(lambda a: lax.dynamic_index_in_dim(a, source, 0, False), gathered)
        )

    return lax.fori_loop(0, ahead, one, state)


def contract(pattern, left, right):
    return jnp.einsum(pattern, left, right, precision=HIGH, preferred_element_type=jnp.float32)


def decay_log_values(input_rows, fading_lowering_array, fading_raising_array, feature_fading_speed):
    apply_projection = jnp.dot(
        input_rows, fading_lowering_array, preferred_element_type=jnp.float32
    )
    smoothed_values = jnp.tanh(apply_projection)
    gate_portion = smoothed_values.astype(jnp.bfloat16)
    rank_projection = lax.dot_general(
        gate_portion,
        fading_raising_array,
        (((1,), (1,)), ((), ())),
        preferred_element_type=jnp.float32,
    )
    return (
        smoothed_values,
        gate_portion,
        -feature_fading_speed[None, :] * jnp.exp(rank_projection),
    )


def compose(decays, own_states, backward):

    def advance(carry, member):
        run_decay, run_state = carry
        decay, own_state = member
        return ((run_decay * decay, decay[..., None] * run_state + own_state), carry)

    initial = (
        jnp.ones(decays.shape[1:], jnp.float32),
        jnp.zeros(own_states.shape[1:], jnp.float32),
    )
    return lax.scan(advance, initial, (decays, own_states), reverse=backward)


def follow(earlier, later):
    return (earlier[0] * later[0], later[0][..., None] * earlier[1] + later[1])


def temporal_blend_sublevel(
    acceptor_lines,
    lookups,
    payloads,
    incoming_cotangent,
    fading_exponent,
    reward_by_attender,
    adjacent_shardlink,
):
    inclusive = jnp.cumsum(fading_exponent, axis=1)
    exclusive = inclusive - fading_exponent
    middle = inclusive[:, BLOCK // 2 - 1 : BLOCK // 2]
    overall = inclusive[:, -1]
    entering = jnp.exp(exclusive)
    leaving = jnp.exp(overall[:, None] - inclusive)
    upward = jnp.exp(exclusive - middle)
    downward = jnp.exp(middle - inclusive)
    decays = jnp.exp(overall)
    reached = acceptor_lines * entering
    faded_keys = lookups * leaving
    own_states = contract("nchk,nchv->nhkv", faded_keys, payloads)
    pull_states = contract("nchk,nchv->nhkv", reached, incoming_cotangent)
    starts, block_ends = adjacent_shardlink(decays, own_states, pull_states)
    position = jnp.arange(BLOCK)
    beneath = position[:, None] > position[None, :]
    early_recept = acceptor_lines * upward
    late_keys = lookups * downward
    scores = jnp.where(beneath, contract("nthk,nshk->nhts", early_recept, late_keys), 0.0)
    present_contribution = jnp.sum(acceptor_lines * reward_by_attender * lookups, axis=-1)[
        ..., None
    ]
    blended_response = (
        contract("nhts,nshv->nthv", scores, payloads)
        + present_contribution * payloads
        + contract("nthk,nhkv->nthv", reached, starts)
    )
    grad_start = decays[..., None] * block_ends + pull_states
    products = jnp.where(beneath, contract("nthv,nshv->nhts", incoming_cotangent, payloads), 0.0)
    agreement_verify = jnp.sum(payloads * incoming_cotangent, axis=-1)[..., None]
    memory_acceptors = entering * contract(
        "nhkv,nthv->nthk", starts, incoming_cotangent
    ) + upward * contract("nhts,nshk->nthk", products, late_keys)
    memory_lookup_lines = leaving * contract(
        "nhkv,nthv->nthk", block_ends, payloads
    ) + downward * contract("nhst,nshk->nthk", products, early_recept)
    payload_deriv = (
        contract("nthk,nhkv->nthv", faded_keys, block_ends)
        + contract("nhst,nshv->nthv", scores, incoming_cotangent)
        + present_contribution * incoming_cotangent
    )
    acceptor_deriv = memory_acceptors + reward_by_attender * lookups * agreement_verify
    lookup_deriv = memory_lookup_lines + reward_by_attender * acceptor_lines * agreement_verify
    present_reward_deriv = jnp.sum(acceptor_lines * lookups * agreement_verify, axis=(0, 1))
    coupling = jnp.sum(grad_start * starts, axis=-1)
    change = lookups * memory_lookup_lines - acceptor_lines * memory_acceptors
    fading_deriv = (
        coupling[:, None] + jnp.cumsum(change, axis=1) - change - acceptor_lines * memory_acceptors
    )
    return (
        blended_response,
        acceptor_deriv,
        lookup_deriv,
        payload_deriv,
        fading_deriv,
        present_reward_deriv,
    )


def sublevel_evaluation(
    reshaped_acceptors,
    reshaped_lookups,
    reshaped_payloads,
    reshaped_source,
    incoming_cotangent_reshaped,
    fading_lowering_array,
    fading_raising_array,
    feature_fading_speed,
    present_reward,
    adjacent_shardlink,
):
    smoothed_values, gate_portion, fading_exponent = decay_log_values(
        reshaped_source, fading_lowering_array, fading_raising_array, feature_fading_speed
    )
    tokens, feature_span = reshaped_acceptors.shape
    tiling_arrangement = (tokens // BLOCK, BLOCK, ATTENDER_TOTAL, LANE_TOTAL)
    collected_outcomes = temporal_blend_sublevel(
        reshaped_acceptors.astype(jnp.float32).reshape(tiling_arrangement),
        reshaped_lookups.astype(jnp.float32).reshape(tiling_arrangement),
        reshaped_payloads.astype(jnp.float32).reshape(tiling_arrangement),
        incoming_cotangent_reshaped.astype(jnp.float32).reshape(tiling_arrangement),
        fading_exponent.reshape(tiling_arrangement),
        present_reward.reshape(ATTENDER_TOTAL, LANE_TOTAL),
        adjacent_shardlink,
    )
    (
        blended_response,
        acceptor_deriv,
        lookup_deriv,
        payload_deriv,
        fading_deriv,
        present_reward_deriv,
    ) = collected_outcomes
    slope = fading_deriv.reshape(tokens, feature_span) * fading_exponent
    slope_portion = slope.astype(jnp.bfloat16)
    gate_gradient = jnp.dot(slope_portion, fading_raising_array, preferred_element_type=jnp.float32)
    projection_gradient = (gate_gradient * (1.0 - smoothed_values * smoothed_values)).astype(
        jnp.bfloat16
    )
    input_gradient = lax.dot_general(
        projection_gradient,
        fading_lowering_array,
        (((1,), (1,)), ((), ())),
        preferred_element_type=jnp.float32,
    ).astype(jnp.bfloat16)
    lowering_array_deriv = lax.dot_general(
        reshaped_source,
        projection_gradient,
        (((0,), (0,)), ((), ())),
        preferred_element_type=jnp.float32,
    )
    raising_array_deriv = lax.dot_general(
        slope_portion, gate_portion, (((0,), (0,)), ((), ())), preferred_element_type=jnp.float32
    )
    speed_deriv = jnp.sum(slope, axis=0)

    def flatten(member):
        return member.reshape(tokens, feature_span).astype(jnp.bfloat16)

    return (
        flatten(blended_response),
        flatten(acceptor_deriv),
        flatten(lookup_deriv),
        flatten(payload_deriv),
        input_gradient,
        (
            lowering_array_deriv,
            raising_array_deriv,
            speed_deriv,
            present_reward_deriv.reshape(feature_span),
        ),
    )


def shard_link(decays, own_states, pull_states):
    ahead_total, ahead = compose(decays, own_states, False)
    behind_total, behind = compose(decays, pull_states, True)
    identity = (jnp.ones_like(ahead_total[0]), jnp.zeros_like(ahead_total[1]))
    prior, state_in = carried_in(ahead_total, "seq", follow, identity, False)
    latter, grad_after = carried_in(behind_total, "seq", follow, identity, True)
    starts = ahead[0][..., None] * state_in[None] + ahead[1]
    block_ends = behind[0][..., None] * grad_after[None] + behind[1]
    return (starts, block_ends)


def per_device(
    acceptors,
    lookups,
    payloads,
    lagged_fading_source,
    response_cotangent,
    fading_lowering_array,
    fading_raising_array,
    feature_fading_speed,
    present_reward,
):
    collected_outcomes = sublevel_evaluation(
        acceptors[0],
        lookups[0],
        payloads[0],
        lagged_fading_source[0],
        response_cotangent[0],
        fading_lowering_array,
        fading_raising_array,
        feature_fading_speed,
        present_reward,
        shard_link,
    )
    sums = collected_outcomes[5]
    dp_count = lax.axis_size("dp")
    share_rows = fading_lowering_array.shape[0] // dp_count
    whole = lax.psum((sums[0], sums[1], sums[2], sums[3]), ("seq", "dp"))
    offset = lax.axis_index("dp") * share_rows
    reduced = tuple((lax.dynamic_slice_in_dim(member, offset, share_rows, 0) for member in whole))
    return (
        collected_outcomes[0][None],
        collected_outcomes[1][None],
        collected_outcomes[2][None],
        collected_outcomes[3][None],
        collected_outcomes[4][None],
        reduced[0],
        reduced[1],
        reduced[2],
        reduced[3],
    )


def solution(mesh):
    in_specs = (
        P("dp", "seq", None),
        P("dp", "seq", None),
        P("dp", "seq", None),
        P("dp", "seq", None),
        P("dp", "seq", None),
        P(),
        P(),
        P(),
        P(),
    )
    out_specs = (
        P("dp", "seq", None),
        P("dp", "seq", None),
        P("dp", "seq", None),
        P("dp", "seq", None),
        P("dp", "seq", None),
        P("dp", None),
        P("dp", None),
        P("dp"),
        P("dp"),
    )
    return jax.shard_map(
        per_device, mesh=mesh, in_specs=in_specs, out_specs=out_specs, check_vma=False
    )
```

profile of v0, /device:TPU:0, one launch (start us, length us, event | category | flops | bytes accessed | tf_op | source)
XLA Modules:
  0.0 555.2 jit_solution(3904437213683768561)
XLA Ops:
  22.7 3.2 copy.93
  28.6 5.5 fusion.57
  36.0 17.7 %while.66 = (s32[]{:T(128)}, f32[40,64]{1,0:T(8,128)S(1)}, f32[40,64,64]{2,1,0:T(8,128)}, f32[2,40,64]{2,1,0:T(8,128)S(1)}, f32[2,40,64,64]{2,3,1,0:T(8,128)}, /...) while((s32[]{:T(128)}, f32[40,64]{1,0:T(8,128)S(1)}, ...), condition=%wide.region_3.4_spmd.clone, body=%wide.region_2.3_spmd.clone.sunk | while | flops 499203 | bytes 6646389 | solution.py:64
  36.0 3.2 select_bitcast_fusion.4
  44.7 3.6 select_bitcast_fusion.4
  54.2 3.3 copy.90
  63.0 3.5 copy.91
  66.4 7.1 %fusion.50 = f32[2,40,64,64]{2,3,1,0:T(8,128)} fusion(f32[2,64,40,64]{1,3,2,0:T(8,128)} %copy.91, bf16[2,64,40,64]{3,2,1,0:T(8,128)(2,1)} %reshape.125, f32[2,64,40,64]{1,3,2,0:T(8,128)S(1)} %copy.89, f32[2,64,40,64]{1,3,2,0:T(8,128)} %copy.90), kind=kOutput, calls=%fused_computation.85 | convolution fusion | flops 252313600 | bytes 5898240 | tf_op jit(solution)/shard_map/nchk,nchv->nhkv/dot_general | solution.py:31
  75.9 29.7 %while.67 = (s32[]{:T(128)}, f32[40,64]{1,0:T(8,128)S(1)}, f32[40,64,64]{2,1,0:T(8,128)}, f32[2,40,64]{2,1,0:T(8,128)}, f32[2,40,64,64]{2,3,1,0:T(8,128)}, /*ind...) while((s32[]{:T(128)}, f32[40,64]{1,0:T(8,128)S(1)}, ...), condition=%wide.region_8.9_spmd.clone, body=%wide.region_7.8_spmd.clone.sunk | while | flops 499204 | bytes 9257093 | solution.py:64
  81.9 3.3 select_bitcast_fusion.5
  96.6 3.7 select_bitcast_fusion.5
  106.4 3.1 fusion.5
  116.5 27.7 %all-gather = f32[640,64]{1,0:T(8,128)} all-gather(f32[40,64]{1,0:T(8,128)S(1)} %get-tuple-element.322), channel_id=2, replica_groups=mesh['seq'=16,'dp'=2] {'seq'}, dimensions={0}, use_global_device_ids=true | all-gather | bytes 174080 | tf_op jit(solution)/shard_map/all_gather | solution.py:18
  144.2 21.9 %all-gather.2 = f32[640,64]{1,0:T(8,128)} all-gather(f32[40,64]{1,0:T(8,128)S(1)} %get-tuple-element.327), channel_id=4, replica_groups=mesh['seq'=16,'dp'=2] {'seq'}, dimensions={0}, use_global_device_ids=true | all-gather | bytes 174080 | tf_op jit(solution)/shard_map/all_gather | solution.py:18
  168.9 4.1 fusion.62
  173.1 7.7 %fusion.52 = f32[2,40,64,64]{3,2,1,0:T(8,128)} fusion(f32[2,64,40,64]{1,3,2,0:T(8,128)S(1)} %copy-done.3, f32[2,64,40,64]{1,3,2,0:T(8,128)S(1)} %copy.89, f32[2,40,64]{2,1,0:T(8,128)S(1)} %get-tuple-element.494, f32[2,64,40,64]{1,3,2,0:T(8,128)S(1)} %copy-done.6, f32[2,64,40,64]{1,3,2,0:T(8,128)S(1)} %copy-done.1), kind=kOutput, calls=%fused_computation.86 | convolution fusion | flops 253296640 | bytes 6574080 | tf_op jit(solution)/shard_map/nthk,nshk->nhts/dot_general | solution.py:31
  185.0 96.9 %all-gather.9.cloned.1.call-done = f32[640,64,64]{2,1,0:T(8,128)} async-done(((f32[40,64,64]{2,1,0:T(8,128)}), f32[640,64,64]{2,1,0:T(8,128)}) %all-gather.9.cloned.1.call-update) | async-done | bytes 10485776 | tf_op jit(solution)/shard_map/all_gather | solution.py:18
  283.1 60.2 %while.65 = (s32[]{:T(128)}, f32[40,64,64]{2,1,0:T(8,128)}, s32[]{:T(128)}, f32[16,40,64]{2,1,0:T(8,128)}, f32[16,40,64,64]{3,2,1,0:T(8,128)}, /*index=5*/s32[]{:T(128)}, s32[]{:T(128)}, s32[]{:T(128)}, s32[]{:T(128)}) while((s32[]{:T(128)}, f32[40,64,64]{2,1,0:T(8,128)}, s32[]{:T(128)}, f32[16,40,64]{2,1,0:T(8,128)}, ...), condition=%wide.region_10.11_spmd, body=%wide.region_9.10_spmd.sunk | while | flops 327686 | bytes 1996947 | solution.py:27
  283.8 3.3 bitcast_add_fusion.8
  287.8 3.3 bitcast_add_fusion.8
  291.8 3.3 bitcast_add_fusion.8
  295.8 3.3 bitcast_add_fusion.8
  299.8 3.3 bitcast_add_fusion.8
  303.8 3.3 bitcast_add_fusion.8
  307.9 3.3 bitcast_add_fusion.8
  311.9 3.3 bitcast_add_fusion.8
  315.9 3.3 bitcast_add_fusion.8
  319.9 3.3 bitcast_add_fusion.8
  323.9 3.3 bitcast_add_fusion.8
  327.9 3.3 bitcast_add_fusion.8
  331.9 3.3 bitcast_add_fusion.8
  335.9 3.3 bitcast_add_fusion.8
  339.9 3.3 bitcast_add_fusion.8
  346.0 6.4 %fusion.24 = f32[2,40,64,64]{3,2,1,0:T(8,128)} fusion(f32[2,40,64,64]{2,3,1,0:T(8,128)} %get-tuple-element.330, f32[40,64,64]{1,2,0:T(8,128)} %copy.119, f32[2,40,64]{2,1,0:T(8,128)S(1)} %copy-done.23, bf16[2,64,40,64]{3,2,1,0:T(8,128)(2,1)} %reshape.124), kind=kOutput, calls=%fused_computation.64 | convolution fusion | flops 252313600 | bytes 3952640 | tf_op jit(solution)/shard_map/nhkv,nthv->nthk/dot_general | solution.py:31
  352.5 4.1 multiply_reduce_fusion
  359.9 6.5 %fusion.9 = f32[2,64,40,64]{1,3,2,0:T(8,128)} fusion(f32[2,40,64,64]{3,2,1,0:T(8,128)S(1)} %fusion.21, f32[2,40,64,64]{3,2,1,0:T(8,128)S(1)} %copy-done.16, f32[2,40,64]{2,1,0:T(8,128)S(1)} %get-tuple-element.494, pred[64,64]{1,0:T(8,128)(4,1)S(1)} %iota_compare_fusion, f32[2,64,40,64]{1,3,2,0:T(8,128)S(1)} %copy-done.4, f32[2,64,40,64]{1,3,2,0:T(8,128)S(1)} %copy.89, ...), kind=kOutput, calls=%fused_computation.36 | convolution fusion | flops 254279680 | bytes 7888896 | tf_op jit(solution)/shard_map/nhts,nshk->nthk/dot_general | solution.py:31
  366.4 11.1 %multiply_subtract_fusion = (f32[2,64,40,64]{1,3,2,0:T(8,128)}, f32[2,64,40,64]{1,3,2,0:T(8,128)}, bf16[2,64,40,64]{1,3,2,0:T(8,128)(2,1)}, bf16[2,64,40,64]{1,3,2,0:T(8,128)(2,1)}, f32[2,64,40]{1,2,0:T(8,128)}) fusion(f32[2,64,40,64]{1,3,2,0:T(8,128)S(1)} %copy-done.4, f32[2,64,40,64]{1,3,2,0:T(8,128)S(1)} %copy-done.7, f32[2,64,40,64]{1,3,2,0:T(8,128)} %fusion.9, ...), kind=kOutput, calls=%fused_computation.39 | convolution fusion | flops 258862080 | bytes 13203456 | tf_op jit(solution)/shard_map/nhst,nshk->nthk/dot_general | solution.py:31
  377.5 3.2 copy.131
  380.7 3.5 fusion.83
  384.2 3.2 copy.132
  387.4 5.0 subtract_subtract_fusion
  392.4 3.3 copy.133
  402.8 6.6 %fusion.23 = f32[2,40,64,64]{2,3,1,0:T(8,128)} fusion(f32[2,40,64,64]{2,3,1,0:T(8,128)S(1)} %copy-done.13, f32[40,64,64]{1,2,0:T(8,128)S(1)} %copy-done.18, f32[2,40,64]{2,1,0:T(8,128)S(1)} %copy-done.24, f32[2,64,40,64]{1,3,2,0:T(8,128)S(1)} %copy-done.5, f32[2,64,40,64]{1,3,2,0:T(8,128)S(1)} %copy.89, f32[2,40,64]{2,1,0:T(8,128)S(1)} %copy-done.22), kind=kOutput, calls=%fused_computation.63 | convolution fusion | flops 252968960 | bytes 5939200 | tf_op jit(solution)/shard_map/nthk,nhkv->nthv/dot_general | solution.py:31
  411.0 7.4 %fusion.7 = bf16[2,64,40,64]{3,1,2,0:T(8,128)(2,1)} fusion(f32[2,40,64,64]{2,3,1,0:T(8,128)} %fusion.23, f32[2,40,64,64]{3,2,1,0:T(8,128)} %fusion.52, f32[2,64,40]{1,2,0:T(8,128)S(1)} %copy-done.26, pred[64,64]{1,0:T(8,128)(4,1)S(1)} %iota_compare_fusion, bf16[2,64,40,64]{3,2,1,0:T(8,128)(2,1)} %reshape.125), kind=kOutput, calls=%fused_computation.30 | convolution fusion | flops 253624320 | bytes 3956736 | tf_op jit(solution)/shard_map/nhst,nshv->nthv/dot_general | solution.py:31
  418.4 37.6 %all-reduce = (f32[2560]{0:T(1024)S(1)}, f32[2560]{0:T(1024)S(1)}) all-reduce(f32[2560]{0:T(1024)S(1)} %get-tuple-element.492, f32[2560]{0:T(1024)S(1)} %copy-done.29), channel_id=1, replica_groups=mesh['seq'=16,'dp'=2] {'seq','dp'}, use_global_device_ids=true, to_apply=%region_16.17 | all-reduce | flops 5120 | bytes 40960 | tf_op jit(solution)/shard_map/psum | solution.py:251
  457.3 3.2 copy.128
  463.4 8.7 %fusion.22 = f32[2,40,64,64]{2,3,1,0:T(8,128)S(1)} fusion(f32[2,40,64,64]{2,3,1,0:T(8,128)} %get-tuple-element.325, f32[40,64,64]{1,2,0:T(8,128)} %copy.103, f32[2,40,64]{2,1,0:T(8,128)S(1)} %get-tuple-element.321, f32[2,64,40,64]{1,3,2,0:T(8,128)} %copy.91, f32[2,64,40,64]{1,3,2,0:T(8,128)S(1)} %copy.89, f32[2,64,40,64]{1,3,2,0:T(8,128)} %copy.90), kind=kOutput, calls=%fused_computation.62 | convolution fusion | flops 252968960 | bytes 7229440 | tf_op jit(solution)/shard_map/nthk,nhkv->nthv/dot_general | solution.py:31
  485.3 59.7 %all-reduce.4.cloned.1.call-done = (f32[2560,128]{0,1:T(8,128)}, f32[2560,128]{1,0:T(8,128)}) async-done(((f32[2560,128]{0,1:T(8,128)}, f32[2560,128]{1,0:T(8,128)}), (f32[2560,128]{0,1:T(8,128)}, f32[2560,128]{1,0:T(8,128)})) %all-reduce.4.cloned.1.call-update) | async-done | bytes 2621456 | tf_op jit(solution)/shard_map/psum | solution.py:251
  (153 shorter events, 124.0 us)
Async XLA Ops:
  7.2 2.4 copy-start
  7.2 173.6 %all-gather.7.cloned.1.call-start = ((), (), s32[]{:S(2)}) async-start(), calls=%async_computation | async-start | bytes 22282240 | tf_op jit(solution)/shard_map/all_gather | solution.py:18
  12.8 1.5 copy-start.14
  18.9 9.7 %copy-start.21 = (f32[2,40,64]{2,1,0:T(8,128)}, f32[2,40,64]{2,1,0:T(8,128)S(1)}, u32[]{:S(2)}) copy-start(f32[2,40,64]{2,1,0:T(8,128)S(1)} %get-tuple-element.495) | copy-start | bytes 61444
  53.7 228.2 %all-gather.9.cloned.1.call-start = ((), (), s32[]{:S(2)}) async-start(), calls=%async_computation.1 | async-start | bytes 22282240 | tf_op jit(solution)/shard_map/all_gather | solution.py:18
  105.6 439.4 %all-reduce.4.cloned.1.call-start = ((), (), s32[]{:S(2)}) async-start(), calls=%async_computation.2 | async-start | bytes 5242880 | tf_op jit(solution)/shard_map/psum | solution.py:251
  166.2 6.9 %copy-start.6 = (f32[2,64,40,64]{1,3,2,0:T(8,128)S(1)}, f32[2,64,40,64]{1,3,2,0:T(8,128)}, u32[]{:S(2)}) copy-start(f32[2,64,40,64]{1,3,2,0:T(8,128)} %copy.91) | copy-start | bytes 3932164
  168.9 4.1 copy-start.1
  168.9 4.2 copy-start.3
  343.2 2.8 copy-start.23
  346.0 6.4 %copy-start.8 = (f32[2,40,64,64]{2,3,1,0:T(8,128)S(1)}, f32[2,40,64,64]{2,3,1,0:T(8,128)}, u32[]{:S(2)}) copy-start(f32[2,40,64,64]{2,3,1,0:T(8,128)} %get-tuple-element.773) | copy-start | bytes 3932164
  346.0 6.4 %copy-start.11 = (f32[2,40,64,64]{2,3,1,0:T(8,128)S(1)}, f32[2,40,64,64]{2,3,1,0:T(8,128)}, u32[]{:S(2)}) copy-start(f32[2,40,64,64]{2,3,1,0:T(8,128)} %get-tuple-element.325) | copy-start | bytes 3932164
  346.0 6.4 %copy-start.12 = (f32[2,40,64,64]{2,3,1,0:T(8,128)S(1)}, f32[2,40,64,64]{2,3,1,0:T(8,128)}, u32[]{:S(2)}) copy-start(f32[2,40,64,64]{2,3,1,0:T(8,128)} %get-tuple-element.330) | copy-start | bytes 3932164
  352.5 4.1 copy-start.10
  352.5 4.1 copy-start.17
  356.6 2.4 copy-start.2
  356.6 2.5 copy-start.4
  356.6 3.3 copy-start.16
  359.9 6.5 %copy-start.7 = (f32[2,64,40,64]{1,3,2,0:T(8,128)S(1)}, f32[2,64,40,64]{1,3,2,0:T(8,128)}, u32[]{:S(2)}) copy-start(f32[2,64,40,64]{1,3,2,0:T(8,128)} %copy.91) | copy-start | bytes 3932164
  359.9 6.5 %copy-start.22 = (f32[2,40,64]{2,1,0:T(8,128)S(1)}, f32[2,40,64]{2,1,0:T(8,128)}, u32[]{:S(2)}) copy-start(f32[2,40,64]{2,1,0:T(8,128)} %copy-done.21) | copy-start | bytes 61444
  359.9 6.5 %copy-start.25 = (f32[2,64,40]{1,2,0:T(8,128)S(1)}, f32[2,64,40]{1,2,0:T(8,128)}, u32[]{:S(2)}) copy-start(f32[2,64,40]{1,2,0:T(8,128)} %fusion.5) | copy-start | bytes 61444
  384.2 3.2 copy-start.28
  398.7 3.8 copy-start.5
  398.7 3.8 copy-start.13
  398.7 4.1 copy-start.18
  398.7 4.1 copy-start.24
  402.8 6.6 %copy-start.20 = (bf16[1,128,2560]{2,1,0:T(8,128)(2,1)S(1)}, bf16[1,128,2560]{2,1,0:T(8,128)(2,1)}, u32[]{:S(2)}) copy-start(bf16[1,128,2560]{2,1,0:T(8,128)(2,1)} %param.20) | copy-start | bytes 1966084
  409.5 1.4 copy-start.26
  410.9 7.5 %copy-start.29 = (f32[2560]{0:T(1024)S(1)}, f32[2560]{0:T(1024)}, u32[]{:S(2)}) copy-start(f32[2560]{0:T(1024)} %multiply_reduce_fusion.2) | copy-start | bytes 30724
  463.4 8.7 %copy-start.9 = (bf16[2,64,40,64]{3,2,1,0:T(8,128)(2,1)S(1)}, bf16[2,64,40,64]{3,2,1,0:T(8,128)(2,1)}, u32[]{:S(2)}) copy-start(bf16[2,64,40,64]{3,2,1,0:T(8,128)(2,1)} %reshape.124) | copy-start | bytes 1966084
  463.4 8.7 %copy-start.15 = (f32[2,40,64,64]{3,2,1,0:T(8,128)S(1)}, f32[2,40,64,64]{3,2,1,0:T(8,128)}, u32[]{:S(2)}) copy-start(f32[2,40,64,64]{3,2,1,0:T(8,128)} %fusion.52) | copy-start | bytes 3932164
  477.0 3.6 copy-start.19
  545.0 2.3 copy-start.27
Sparse Core Ops, SparseCore 0:
  53.8 117.3 all-gather.6
  172.8 108.9 all-gather.8
  411.0 133.9 all-reduce.3
where the time goes:
time: 564 us; the launch traced here: 555 us
  waiting for transfers between devices  157 us (28%)
  local copies, waits for them, and re-layouts  124 us (22%)
  other arithmetic  87.2 us (15%)
  blocking collectives  87.2 us (15%)
  matrix products  84.5 us (15%)
  between operations  14.5 us (3%)
    all_gather x2, waiting for transfers between devices, carried_in(): gathered = jax.tree.map(lambda a: lax.all_gather(a, axis), part)  96.9 us
    dot_general x12, matrix products, contract(): jnp.einsum(pattern, left, right, precision=HIGH, preferred_element_type=j...  76 us
    psum x1, waiting for transfers between devices, per_device(): whole = lax.psum((sums[0], sums[1], sums[2], sums[3]), ('seq', 'dp'))  59.7 us
    all_gather x2, blocking collectives, carried_in(): gathered = jax.tree.map(lambda a: lax.all_gather(a, axis), part)  49.6 us
    add x15, other arithmetic, follow(): return (earlier[0] * later[0], later[0][..., None] * earlier[1] + later[1])  49.2 us
    psum x1, blocking collectives, per_device(): whole = lax.psum((sums[0], sums[1], sums[2], sums[3]), ('seq', 'dp'))  37.6 us
    dynamic_update_slice x8, local copies, waits for them, and re-layouts, compose(): return lax.scan(advance, initial, (decays, own_states), reverse=backward)  21.4 us
    convert_element_type x8, local copies, waits for them, and re-layouts, flatten(): return member.reshape(tokens, feature_span).astype(jnp.bfloat16)  14.5 us
  transfers between devices with their start and end apart: 3, of which 2 were waited for; matrix products, arithmetic and copies ran while one was open for 21% of the time, Pallas kernels for 0%

commit v1 on v0

v1 whole, which is shorter than its diff:
```python
import functools
import jax
import jax.numpy as jnp
from jax import lax
from jax.experimental import pallas as pl
from jax.experimental.pallas import tpu as pltpu
from jax.sharding import PartitionSpec as P

LANE_TOTAL = 64
BLOCK = 64
PAIR = 2 * LANE_TOTAL
F32 = jnp.float32
BF16 = jnp.bfloat16
GONE = -1e30
SKEW = 4
GRAIN = 512


def nn(a, b):
    return lax.dot_general(a, b, (((1,), (0,)), ((), ())), preferred_element_type=F32)


def nt(a, b):
    return lax.dot_general(a, b, (((1,), (1,)), ((), ())), preferred_element_type=F32)


def tn(a, b):
    return lax.dot_general(a, b, (((0,), (0,)), ((), ())), preferred_element_type=F32)


def split(a, terms):
    out = []
    for _ in range(terms):
        out.append(a.astype(BF16))
        a = a - out[-1].astype(F32)
    return out


def exact_left(m, a, terms):
    return sum(nn(m, t) for t in split(a, terms))


def exact_right(a, m, terms):
    return sum(nn(t, m) for t in split(a, terms))


def triangle(n, strict):
    row = lax.broadcasted_iota(jnp.int32, (n, n), 0)
    col = lax.broadcasted_iota(jnp.int32, (n, n), 1)
    keep = row > col if strict else row >= col
    return jnp.where(keep, 1.0, 0.0).astype(BF16)


def diagonal_heads(m):
    lane = lax.broadcasted_iota(jnp.int32, (LANE_TOTAL, PAIR), 1)
    return jnp.where(lane < LANE_TOTAL, m[:LANE_TOTAL], m[LANE_TOTAL:])


def totals_kernel(
    x_ref, a_ref, b_ref, speed_ref, r_ref, k_ref, v_ref, g_ref,
    th_ref, w_ref, incl_ref, own_ref, pull_ref, dec_ref,
):
    tokens = x_ref.shape[0]

    @pl.when(pl.program_id(0) == 0)
    def _():
        th_ref[...] = jnp.tanh(nn(x_ref[...], a_ref[...]))

    gate = th_ref[...].astype(BF16)
    w = -speed_ref[0] * jnp.exp(nt(gate, b_ref[...]))
    incl = exact_left(triangle(tokens, False), w, 3)
    total = incl[tokens - 1 :]
    w_ref[...] = w
    incl_ref[...] = incl
    faded = k_ref[...].astype(F32) * jnp.exp(total - incl)
    reached = r_ref[...].astype(F32) * jnp.exp(incl - w)
    own_ref[0] = diagonal_heads(sum(tn(v_ref[...], t) for t in split(faded, 2)))
    pull_ref[0] = diagonal_heads(sum(tn(g_ref[...], t) for t in split(reached, 2)))
    dec_ref[0] = jnp.exp(total)


def chain_kernel(own_ref, pull_ref, dec_ref, s_ref, g_ref, so_ref, go_ref, sf, rf, sb, rb):
    n = lax.axis_size("seq")
    me = lax.axis_index("seq")
    pairs = own_ref.shape[0]
    right = lax.rem(me + 1, n)
    left = lax.rem(me + n - 1, n)
    barrier = pltpu.get_barrier_semaphore()
    for neighbour in (left, right):
        pl.semaphore_signal(
            barrier, inc=1, device_id={"seq": neighbour}, device_id_type=pl.DeviceIdType.MESH
        )
    pl.semaphore_wait(barrier, 2)

    def forward(c):
        return pltpu.make_async_remote_copy(
            src_ref=so_ref.at[c], dst_ref=s_ref.at[c], send_sem=sf.at[c], recv_sem=rf.at[c],
            device_id={"seq": right}, device_id_type=pl.DeviceIdType.MESH,
        )

    def backward(c):
        return pltpu.make_async_remote_copy(
            src_ref=go_ref.at[c], dst_ref=g_ref.at[c], send_sem=sb.at[c], recv_sem=rb.at[c],
            device_id={"seq": left}, device_id_type=pl.DeviceIdType.MESH,
        )

    def relay(c, first, last, copy, in_ref, out_ref, add_ref):
        @pl.when((c >= 0) & (c < pairs))
        def _():
            @pl.when(first)
            def _():
                in_ref[c] = jnp.zeros(in_ref.shape[1:], F32)

            @pl.when(jnp.logical_not(first))
            def _():
                copy(c).wait_recv()

            @pl.when(jnp.logical_not(last))
            def _():
                out_ref[c] = dec_ref[c] * in_ref[c] + add_ref[c]
                copy(c).start()

    at_start = me == 0
    at_end = me == n - 1

    def step(s, carry):
        relay(s - SKEW * me, at_start, at_end, forward, s_ref, so_ref, own_ref)
        relay(s - SKEW * (n - 1 - me), at_end, at_start, backward, g_ref, go_ref, pull_ref)
        return carry

    lax.fori_loop(0, SKEW * (n - 1) + pairs, step, 0)

    def finish(c, carry):
        @pl.when(jnp.logical_not(at_end))
        def _():
            forward(c).wait_send()

        @pl.when(jnp.logical_not(at_start))
        def _():
            backward(c).wait_send()

        return carry

    lax.fori_loop(0, pairs, finish, 0)


def finish_kernel(
    x_ref, a_ref, b_ref, u_ref, r_ref, k_ref, v_ref, g_ref,
    th_ref, w_ref, incl_ref, pull_ref, dec_ref, s_ref, ga_ref,
    mixed_ref, dr_ref, dk_ref, dv_ref, dx_ref, sums_ref, db_ref, acc_ref,
):
    tokens, span = x_ref.shape
    pair = pl.program_id(0)
    pairs = pl.num_programs(0)

    @pl.when(pair == 0)
    def _():
        sums_ref[span:, :] = jnp.zeros((sums_ref.shape[0] - span, sums_ref.shape[1]), F32)

    row = lax.broadcasted_iota(jnp.int32, (tokens, PAIR), 0)
    lane = lax.broadcasted_iota(jnp.int32, (tokens, PAIR), 1)
    at = lax.broadcasted_iota(jnp.int32, (tokens, tokens), 0)
    of = lax.broadcasted_iota(jnp.int32, (tokens, tokens), 1)
    near = (at > of) & (at // BLOCK == of // BLOCK)
    far = (at >= BLOCK) & (of < BLOCK)
    low = lane < LANE_TOTAL
    upper = row < BLOCK
    zero = jnp.zeros((tokens, PAIR), BF16)

    def heads(a):
        return jnp.where(low, a, zero), jnp.where(low, zero, a)

    rb, kb, vb, gb = r_ref[...], k_ref[...], v_ref[...], g_ref[...]
    r, k, v, g = rb.astype(F32), kb.astype(F32), vb.astype(F32), gb.astype(F32)
    w, incl = w_ref[...], incl_ref[...]
    u = u_ref[0]
    excl = incl - w
    total = incl[tokens - 1 :]
    half = BLOCK // 2
    middle = jnp.where(upper, incl[half - 1 : half], incl[BLOCK + half - 1 : BLOCK + half])
    edge = incl[BLOCK - 1 : BLOCK]
    upward = jnp.exp(excl - middle)
    downward = jnp.exp(middle - incl)
    entering = jnp.exp(excl)
    leaving = jnp.exp(total - incl)
    past_edge = jnp.exp(jnp.where(upper, GONE, excl - edge))
    to_edge = jnp.exp(jnp.where(upper, edge - incl, GONE))
    early_full = split(r * upward, 2)
    late_full = split(k * downward, 2)
    over_full = split(r * past_edge, 2)
    under_full = split(k * to_edge, 2)
    early, over = heads(early_full[0]), heads(over_full[0])
    late, under = late_full[0], under_full[0]
    v2, g2 = heads(vb), heads(gb)
    reached = (r * entering).astype(BF16)
    faded = (k * leaving).astype(BF16)

    s, ga = s_ref[0], ga_ref[0]
    lane_s = lax.broadcasted_iota(jnp.int32, s.shape, 1) < LANE_TOTAL

    def blocks(a):
        return split(
            jnp.concatenate([jnp.where(lane_s, a, 0.0), jnp.where(lane_s, 0.0, a)], axis=0), 2
        )

    (s_diag, s_rest), (g_diag, g_rest) = blocks(s), blocks(ga)

    def both(pieces, axis):
        return jnp.concatenate(pieces, axis=axis)

    scores, inside, across = [], [], []
    for h in range(2):
        scores.append(
            (jnp.where(near, nt(early[h], late), 0.0) + nt(over[h], under)).astype(BF16)
        )
        product = nt(g2[h], vb)
        inside.append(split(jnp.where(near, product, 0.0), 2))
        across.append(split(jnp.where(far, product, 0.0), 2))

    ones = jnp.where(
        (lax.broadcasted_iota(jnp.int32, (PAIR, PAIR), 0) // LANE_TOTAL)
        == (lax.broadcasted_iota(jnp.int32, (PAIR, PAIR), 1) // LANE_TOTAL),
        1.0, 0.0,
    ).astype(BF16)
    present = exact_right(r * u * k, ones, 2)
    agree = exact_right(v * g, ones, 2)

    v_stack, g_stack = both(v2, 0), both(g2, 0)
    mixed = nn(both(scores, 1), v_stack) + nt(reached, s_diag) + present * v
    dv = tn(both(scores, 0), g_stack) + nt(faded, g_diag) + present * g
    def thrice(product, left, right_terms):
        high, rest = (both([product[0][i], product[1][i]], left) for i in range(2))
        main, less = (both(heads(t), 0) for t in right_terms)
        multiply = nn if left == 1 else tn
        return multiply(high, main) + multiply(rest, main) + multiply(high, less)

    memory_r = (
        entering * (nn(gb, s_diag) + nn(gb, s_rest))
        + upward * thrice(inside, 1, late_full)
        + past_edge * thrice(across, 1, under_full)
    )
    memory_k = (
        leaving * (nn(vb, g_diag) + nn(vb, g_rest))
        + downward * thrice(inside, 0, early_full)
        + to_edge * thrice(across, 0, over_full)
    )
    mixed_ref[...] = mixed.astype(BF16)
    dv_ref[...] = dv.astype(BF16)
    dr_ref[...] = (memory_r + u * k * agree).astype(BF16)
    dk_ref[...] = (memory_k + u * r * agree).astype(BF16)
    sums_ref[pl.ds(span + pairs + pair, 1), :] = jnp.sum(r * k * agree, axis=0, keepdims=True)
    coupling = jnp.sum((dec_ref[0] * ga + pull_ref[0]) * s, axis=0, keepdims=True)
    pulled = r * memory_r
    change = k * memory_k - pulled
    fading = coupling + exact_left(triangle(tokens, True), change, 2) - pulled
    slope = fading * w
    sums_ref[pl.ds(span + pair, 1), :] = jnp.sum(slope, axis=0, keepdims=True)
    slope_half = slope.astype(BF16)
    th = th_ref[...]
    db_ref[...] = tn(slope_half, th.astype(BF16))
    back = nn(slope_half, b_ref[...])

    @pl.when(pair == 0)
    def _():
        acc_ref[...] = back

    @pl.when(pair > 0)
    def _():
        acc_ref[...] += back

    @pl.when(pair == pairs - 1)
    def _():
        grad = (acc_ref[...] * (1.0 - th * th)).astype(BF16)

        def part(i, carry):
            c = pl.ds(pl.multiple_of(i * PAIR, PAIR), PAIR)
            dx_ref[:, c] = nt(grad, a_ref[c, :]).astype(BF16)
            sums_ref[c, :] = tn(x_ref[:, c], grad)
            return carry

        lax.fori_loop(0, span // PAIR, part, 0)


def per_device(r, k, v, x, g, a, b, speed, reward):
    r, k, v, x, g = r[0], k[0], v[0], x[0], g[0]
    tokens, span = r.shape
    rank = a.shape[1]
    pairs = span // PAIR
    speed, reward = speed.reshape(pairs, 1, PAIR), reward.reshape(pairs, 1, PAIR)
    whole = lambda shape: pl.BlockSpec(shape, lambda i: (0,) * len(shape))
    cols = pl.BlockSpec((tokens, PAIR), lambda i: (0, i))
    rows = pl.BlockSpec((PAIR, rank), lambda i: (i, 0))
    state = pl.BlockSpec((1, LANE_TOTAL, PAIR), lambda i: (i, 0, 0))
    thin = pl.BlockSpec((1, 1, PAIR), lambda i: (i, 0, 0))
    f32 = lambda *shape: jax.ShapeDtypeStruct(shape, F32)
    b16 = lambda *shape: jax.ShapeDtypeStruct(shape, BF16)
    states = f32(pairs, LANE_TOTAL, PAIR)
    th, w, incl, own, pull, dec = pl.pallas_call(
        totals_kernel,
        grid=(pairs,),
        in_specs=[whole(x.shape), whole(a.shape), rows, thin, cols, cols, cols, cols],
        out_specs=[whole((tokens, rank)), cols, cols, state, state, thin],
        out_shape=[
            f32(tokens, rank), f32(tokens, span), f32(tokens, span), states, states,
            f32(pairs, 1, PAIR),
        ],
        name="totals",
    )(x, a, b, speed, r, k, v, g)
    vmem = pl.BlockSpec(memory_space=pltpu.VMEM)
    dma = pltpu.SemaphoreType.DMA((pairs,))
    s_in, g_after = pl.pallas_call(
        chain_kernel,
        in_specs=[vmem] * 3,
        out_specs=[vmem] * 2,
        out_shape=[states, states],
        scratch_shapes=[
            pltpu.VMEM(states.shape, F32), pltpu.VMEM(states.shape, F32), dma, dma, dma, dma,
        ],
        compiler_params=pltpu.CompilerParams(collective_id=0, has_side_effects=True),
        name="chain",
    )(own, pull, dec)
    height = -(-(span + 2 * pairs) // GRAIN) * GRAIN
    mixed, dr, dk, dv, dx, sums, db = pl.pallas_call(
        finish_kernel,
        grid=(pairs,),
        in_specs=[
            whole(x.shape), whole(a.shape), rows, thin, cols, cols, cols, cols,
            whole((tokens, rank)), cols, cols, state, thin, state, state,
        ],
        out_specs=[
            cols, cols, cols, cols, whole((tokens, span)), whole((height, rank)), rows,
        ],
        out_shape=[
            b16(tokens, span), b16(tokens, span), b16(tokens, span), b16(tokens, span),
            b16(tokens, span), f32(height, rank), f32(span, rank),
        ],
        scratch_shapes=[pltpu.VMEM((tokens, rank), F32)],
        name="finish",
    )(x, a, b, reward, r, k, v, g, th, w, incl, pull, dec, s_in, g_after)

    dp = lax.axis_size("dp")
    place = lax.axis_index("dp")
    first, second = lax.psum((sums, db), ("seq", "dp"))

    def share(array, start, count):
        return lax.dynamic_slice_in_dim(array, start + place * (count // dp), count // dp, 0)

    ga, gb = share(first, 0, span), share(second, 0, span)
    gw = share(first, span, pairs).reshape(span // dp)
    gu = share(first, span + pairs, pairs).reshape(span // dp)
    return (mixed[None], dr[None], dk[None], dv[None], dx[None], ga, gb, gw, gu)


def solution(mesh):
    split_rows = P("dp", "seq", None)
    in_specs = (split_rows,) * 5 + (P(),) * 4
    out_specs = (split_rows,) * 5 + (P("dp", None), P("dp", None), P("dp"), P("dp"))
    return jax.shard_map(
        per_device, mesh=mesh, in_specs=in_specs, out_specs=out_specs, check_vma=False
    )
```

time: 564 us -> 253 us (0.45); the launches traced: 555 us -> 251 us
  local copies, waits for them, and re-layouts: 124 us -> 6.44 us
  Pallas kernels: 0 us -> 92.9 us
  other arithmetic: 87.2 us -> 0 us
  blocking collectives: 87.2 us -> 0 us
  matrix products: 84.5 us -> 0 us
  waiting for transfers between devices: 157 us -> 138 us
    all_gather x2 -> x0, waiting for transfers between devices: 96.9 us -> none  [carried_in(): gathered = jax.tree.map(lambda a: lax.all_gather(a, axis), part)]
    pallas_call x0 -> x3, Pallas kernels: none -> 92.9 us  [the longest x1 46.1 us: per_device(): pl.pallas_call(chain_kernel, in_specs=[vmem] * 3, out_specs=[vmem] * 2, o...]
    dot_general x18 -> x0, matrix products: 84.5 us -> none  [the longest x12 76 us: contract(): jnp.einsum(pattern, left, right, precision=HIGH, preferred_element_type=j...]
    psum x1, waiting for transfers between devices: 59.7 us -> 138 us  [per_device(): first, second = lax.psum((sums, db), ('seq', 'dp'))]
    all_gather x2 -> x0, blocking collectives: 49.6 us -> none  [carried_in(): gathered = jax.tree.map(lambda a: lax.all_gather(a, axis), part)]
    add x15 -> x0, other arithmetic: 49.2 us -> none  [follow(): return (earlier[0] * later[0], later[0][..., None] * earlier[1] + later[1])]
    psum x1 -> x0, blocking collectives: 37.6 us -> none  [per_device(): whole = lax.psum((sums[0], sums[1], sums[2], sums[3]), ('seq', 'dp'))]
    convert_element_type x12 -> x0, local copies, waits for them, and re-layouts: 27 us -> none  [the longest x8 14.5 us: flatten(): return member.reshape(tokens, feature_span).astype(jnp.bfloat16)]
  transfers between devices with their start and end apart: 3 -> 1, of which waited for: 2 -> 1; matrix products, arithmetic and copies ran while one was open for 21% -> 0% of each run, Pallas kernels for 0% -> 0%
where the time goes in v1:
time: 253 us; the launch traced here: 251 us
  waiting for transfers between devices  138 us (55%)
  Pallas kernels  92.9 us (37%)
  between operations  14.1 us (6%)
  local copies, waits for them, and re-layouts  6.44 us (3%)
    psum x1, waiting for transfers between devices, per_device(): first, second = lax.psum((sums, db), ('seq', 'dp'))  138 us
    pallas_call x1, Pallas kernels, per_device(): pl.pallas_call(chain_kernel, in_specs=[vmem] * 3, out_specs=[vmem] * 2, o...  46.1 us
    pallas_call x1, Pallas kernels, per_device(): pl.pallas_call(finish_kernel, grid=(pairs,), in_specs=[whole(x.shape), wh...  30.3 us
    pallas_call x1, Pallas kernels, per_device(): pl.pallas_call(totals_kernel, grid=(pairs,), in_specs=[whole(x.shape), wh...  16.4 us
  transfers between devices with their start and end apart: 1, of which 1 were waited for; matrix products, arithmetic and copies ran while one was open for 0% of the time, Pallas kernels for 0%

profile of v1, /device:TPU:0, one launch (start us, length us, event | category | flops | bytes accessed | tf_op | source)
XLA Modules:
  0.0 251.3 jit_solution(8218425329343044507)
XLA Ops:
  7.2 0.0 all-reduce.3.cloned.1.call-start
  7.2 1.3 reshape.31.speed_ref
  8.5 1.3 reshape.30.u_ref
  9.9 16.4 %totals.1 = (f32[128,128]{1,0:T(8,128)}, f32[128,2560]{1,0:T(8,128)}, f32[128,2560]{1,0:T(8,128)}, f32[20,64,128]{2,1,0:T(8,128)}, f32[20,64,128]{2,1,0:T(8,128)}, /*index=5*/f32[20,1,128]{2,1,0:T(1,128)}) custom-call(bf16[128,2560]{1,0:T(8,128)(2,1)} %bitcast.14, bf16[2560,128]{1,0:T(8,128)(2,1)} %a_ref.3, bf16[2560,128]{1,0:T(8,128)(2,1)} %b_ref.3, ...), custom_call_target="tpu_custom_call" | custom-call | tf_op jit(solution)/shard_map/totals/pallas_call | solution.py:298
  26.3 46.1 %chain.1 = (f32[20,64,128]{2,1,0:T(8,128)}, f32[20,64,128]{2,1,0:T(8,128)}) custom-call(f32[20,64,128]{2,1,0:T(8,128)} %get-tuple-element.29.own_ref, f32[20,64,128]{2,1,0:T(8,128)} %get-tuple-element.27.pull_ref, f32[20,1,128]{2,1,0:T(1,128)} %get-tuple-element.28.dec_ref), custom_call_target="tpu_custom_call" | custom-call | tf_op jit(solution)/shard_map/chain/pallas_call | solution.py:311
  72.4 30.3 %finish.1 = (bf16[128,2560]{1,0:T(8,128)(2,1)}, bf16[128,2560]{1,0:T(8,128)(2,1)}, bf16[128,2560]{1,0:T(8,128)(2,1)}, bf16[128,2560]{1,0:T(8,128)(2,1)}, bf16[12...) custom-call(bf16[128,2560]{1,0:T(8,128)(2,1)} %bitcast.15, bf16[2560,128]{1,0:T(8,128)(2,1)} %a_ref.3, ...), custom_call_target="tpu_custom_call" | custom-call | tf_op jit(solution)/shard_map/finish/pallas_call | solution.py:323
  102.8 0.0 all-reduce.3.cloned.1.call-update
  102.8 137.8 %all-reduce.3.cloned.1.call-done = (f32[3072,128]{1,0:T(8,128)}, f32[2560,128]{1,0:T(8,128)}) async-done(((f32[3072,128]{1,0:T(8,128)}, f32[2560,128]{1,0:T(8,128)}), (f32[3072,128]{1,0:T(8,128)}, f32[2560,128]{1,0:T(8,128)})) %all-reduce.3.cloned.1.call-update) | async-done | bytes 2883600 | tf_op jit(solution)/shard_map/psum | solution.py:343
  240.6 1.4 dynamic-slice_bitcast_fusion
  242.0 2.4 constant_dynamic-slice_fusion
Async XLA Ops:
  7.2 233.5 %all-reduce.3.cloned.1.call-start = ((), (), s32[]{:S(2)}) async-start(), calls=%async_computation | async-start | bytes 5767168 | tf_op jit(solution)/shard_map/psum | solution.py:343
Sparse Core Ops, SparseCore 0:
  102.9 137.6 all-reduce.2
